TPU v7x, 32 devices: a whole 2x2x4 slice. The times are simulated.
32 devices in a mesh: aa: 8 (over z, x), ba: 4 (over y, core).
Axes of the slice: x: 2, y: 2, z: 4, core: 2. Of those that a mesh axis runs over, the one named last changes fastest.
Arguments:
- grid_features: bfloat16 [128, 128, 256, 128], P('aa', 'ba'), may hold values from -6 to 6
- weight_real: bfloat16 [32, 32, 16, 128, 128], P('ba', None, 'aa'), may hold values from -6 to 6
- weight_imag: bfloat16 [32, 32, 16, 128, 128], P('ba', None, 'aa'), may hold values from -6 to 6
- mode_keep: int32 [32, 16], P('ba', 'aa'), may hold values from 1 to 16, as said below
- local_weight: bfloat16 [128, 128], replicated, may hold values from -0.5 to 0.5
- local_bias: bfloat16 [128], replicated, may hold values from -3 to 3
Outputs:
- layer_output: bfloat16 [128, 128, 256, 128], P('aa', 'ba')
Inputs may be any that keep to these rules, and one draw needn't show every extreme that they name: mode_keep[i, k] counts the retained levels of the second frequency on the line of the i-th retained first frequency and the k-th third frequency.
All inputs are finite; a program needn't handle non-finite values.
Results may differ from a plain program's by a relative error of at most 0.012.
Values may be sent and summed in bfloat16 or wider, within the bound.
No kernel may reach another device: no remote copies, remote signals or barrier semaphores. Data moves between devices by JAX's collectives and lax.ppermute only.
A program may use at most 256 MiB of HBM per device.

v0:
```python
import math

import jax
import jax.numpy as jnp
from jax import lax
from jax.sharding import PartitionSpec as P

NX = 128
NY = 128
NZ = 256
KX = 32
KY = 32
KZ = 16


highest = lax.Precision.HIGHEST


def kept_modes(length, number):
    positions = jnp.arange(number, dtype=jnp.int32)
    return jnp.where(positions < number // 2, positions, positions + (length - number))


def phase_tables(length, mode_list):
    places = jnp.arange(length, dtype=jnp.int32)
    phase_steps = places[:, None] * mode_list[None, :] % length
    angles = phase_steps.astype(jnp.float32) * (2.0 * math.pi / length)
    return (jnp.cos(angles), jnp.sin(angles))


def forward_kernel(length, number):
    cosine_table, sine_table = phase_tables(length, kept_modes(length, number))
    upper_rows = jnp.concatenate([cosine_table, -sine_table], axis=1)
    lower_rows = jnp.concatenate([sine_table, cosine_table], axis=1)
    return jnp.concatenate([upper_rows, lower_rows], axis=0)


def inverse_kernel(length, number):
    cosine_table, sine_table = phase_tables(length, kept_modes(length, number))
    upper_rows = jnp.concatenate([cosine_table.T, sine_table.T], axis=1)
    lower_rows = jnp.concatenate([-sine_table.T, cosine_table.T], axis=1)
    return jnp.concatenate([upper_rows, lower_rows], axis=0)


def depth_kernels():
    cosine_table, sine_table = phase_tables(NZ, jnp.arange(KZ, dtype=jnp.int32))
    forward = jnp.concatenate([cosine_table, -sine_table], axis=1).astype(jnp.bfloat16)
    factor = jnp.where(jnp.arange(KZ, dtype=jnp.int32) == 0, 1.0, 2.0).astype(jnp.float32) / (
        NX * NY * NZ
    )
    inverse = jnp.concatenate(
        [cosine_table.T * factor[:, None], -sine_table.T * factor[:, None]], axis=0
    ).astype(jnp.bfloat16)
    return (forward, inverse)


def along_first(operand, kernel):
    return jnp.einsum(
        "pabc,pq->qabc", operand, kernel, precision=highest, preferred_element_type=jnp.float32
    )


def along_second(operand, kernel):
    return jnp.einsum(
        "apbc,pq->aqbc", operand, kernel, precision=highest, preferred_element_type=jnp.float32
    )


def mode_mask(kept_counts):
    positions = jnp.arange(KY, dtype=jnp.int32)
    levels = jnp.where(positions < KY // 2, positions, KY - 1 - positions)
    return (levels[None, :, None] < kept_counts[:, None, :]).astype(jnp.float32)


def mix_modes(spec_real, spec_imag, weight_real, weight_imag, kept_counts):
    pattern = "abcd,abcde->abce"
    out_real = jnp.einsum(
        pattern, spec_real, weight_real, preferred_element_type=jnp.float32
    ) - jnp.einsum(pattern, spec_imag, weight_imag, preferred_element_type=jnp.float32)
    out_imag = jnp.einsum(
        pattern, spec_real, weight_imag, preferred_element_type=jnp.float32
    ) + jnp.einsum(pattern, spec_imag, weight_real, preferred_element_type=jnp.float32)
    keep_mask = mode_mask(kept_counts)[..., None]
    return (out_real * keep_mask, out_imag * keep_mask)


def per_device(grid_features, weight_real, weight_imag, mode_keep, local_weight, local_bias):
    forward_depth, inverse_depth = depth_kernels()
    coeffs = jnp.einsum(
        "xyzc,zk->xykc", grid_features, forward_depth, preferred_element_type=jnp.float32
    ).astype(jnp.bfloat16)
    depth_real = coeffs[:, :, :KZ]
    depth_imag = coeffs[:, :, KZ:]
    gathered = (
        lax.all_to_all(depth_real, "aa", split_axis=2, concat_axis=0, tiled=True),
        lax.all_to_all(depth_imag, "aa", split_axis=2, concat_axis=0, tiled=True),
    )
    result = along_first(
        jnp.concatenate(gathered, axis=0).astype(jnp.float32), forward_kernel(NX, KX)
    )
    gathered = (
        lax.all_to_all(
            result[:KX].astype(jnp.bfloat16), "ba", split_axis=0, concat_axis=1, tiled=True
        ).astype(jnp.float32),
        lax.all_to_all(
            result[KX:].astype(jnp.bfloat16), "ba", split_axis=0, concat_axis=1, tiled=True
        ).astype(jnp.float32),
    )
    result = along_second(jnp.concatenate(gathered, axis=1), forward_kernel(NY, KY)).astype(
        jnp.bfloat16
    )
    mixed_real, mixed_imag = mix_modes(
        result[:, :KY], result[:, KY:], weight_real, weight_imag, mode_keep
    )
    result = along_second(jnp.concatenate([mixed_real, mixed_imag], axis=1), inverse_kernel(NY, KY))
    gathered = (
        lax.all_to_all(
            result[:, :NY].astype(jnp.bfloat16), "ba", split_axis=1, concat_axis=0, tiled=True
        ).astype(jnp.float32),
        lax.all_to_all(
            result[:, NY:].astype(jnp.bfloat16), "ba", split_axis=1, concat_axis=0, tiled=True
        ).astype(jnp.float32),
    )
    result = along_first(jnp.concatenate(gathered, axis=0), inverse_kernel(NX, KX)).astype(
        jnp.bfloat16
    )
    back_field = (
        lax.all_to_all(result[:NX], "aa", split_axis=0, concat_axis=2, tiled=True),
        lax.all_to_all(result[NX:], "aa", split_axis=0, concat_axis=2, tiled=True),
    )
    spectral = jnp.einsum(
        "xykc,kz->xyzc",
        jnp.concatenate(back_field, axis=2),
        inverse_depth,
        preferred_element_type=jnp.float32,
    )
    local_term = jnp.einsum(
        "xyzc,cd->xyzd", grid_features, local_weight, preferred_element_type=jnp.float32
    )
    return jax.nn.gelu(spectral + local_term + local_bias.astype(jnp.float32)).astype(jnp.bfloat16)


def solution(mesh):
    in_specs = (
        P("aa", "ba", None, None),
        P("ba", None, "aa", None, None),
        P("ba", None, "aa", None, None),
        P("ba", "aa"),
        P(),
        P(),
    )
    out_specs = P("aa", "ba", None, None)
    return jax.shard_map(
        per_device, mesh=mesh, in_specs=in_specs, out_specs=out_specs, check_vma=False
    )
```

profile of v0, /device:TPU:0, one launch (start us, length us, event | category | flops | bytes accessed | tf_op | source)
XLA Modules:
  0.0 419.5 jit_solution(7839791159601582577)
XLA Ops:
  0.1 18.5 %convert_bitcast_fusion = bf16[16,32,32,128]{3,2,1,0:T(8,128)(2,1)} fusion(bf16[16,32,256,128]{3,2,1,0:T(8,128)(2,1)} %param.6, bf16[256,16]{0,1:T(8,128)(2,1)S(1)} %get-tuple-element.25, bf16[256,16]{0,1:T(8,128)(2,1)S(1)} %get-tuple-element.26), kind=kOutput, calls=%fused_computation.19 | convolution fusion | flops 1075871744 | bytes 37765120 | tf_op jit(solution)/shard_map/xyzc,zk->xykc/dot_general | solution.py:89
  18.6 4.5 %fusion.87 = (bf16[16,32,16,128]{3,2,1,0:T(8,128)(2,1)S(1)}, bf16[16,32,16,128]{3,2,1,0:T(8,128)(2,1)}) fusion(bf16[16,32,32,128]{3,2,1,0:T(8,128)(2,1)} %convert_bitcast_fusion), kind=kLoop, calls=%fused_computation.122 | loop fusion | bytes 8388608 | tf_op jit(solution)/shard_map/slice | solution.py:92
  25.0 7.3 %all-to-all-start = ((bf16[16,32,16,128]{3,1,0,2:T(8,128)(2,1)}), bf16[16,32,16,128]{3,1,0,2:T(8,128)(2,1)S(1)}, u32[]{:S(2)}, u32[]{:S(2)}) async-start(bf16[16,32,16,128]{3,1,0,2:T(8,128)(2,1)} %copy.16), calls=%async_computation | async-start | bytes 4194304 | tf_op jit(solution)/shard_map/all_to_all | solution.py:95
  32.2 3.5 copy.18
  35.7 44.8 %all-to-all-done = bf16[16,32,16,128]{3,1,0,2:T(8,128)(2,1)S(1)} async-done(((bf16[16,32,16,128]{3,1,0,2:T(8,128)(2,1)}), bf16[16,32,16,128]{3,1,0,2:T(8,128)(2,1)S(1)}, u32[]{:S(2)}, u32[]{:S(2)}) %all-to-all-start) | async-done | bytes 2097184 | tf_op jit(solution)/shard_map/all_to_all | solution.py:95
  80.5 4.4 %all-to-all-start.1 = ((bf16[16,32,16,128]{3,1,0,2:T(8,128)(2,1)}), bf16[16,32,16,128]{3,1,0,2:T(8,128)(2,1)}, u32[]{:S(2)}, u32[]{:S(2)}) async-start(bf16[16,32,16,128]{3,1,0,2:T(8,128)(2,1)} %copy.18), calls=%async_computation.1 | async-start | bytes 4194304 | tf_op jit(solution)/shard_map/all_to_all | solution.py:96
  87.2 45.5 %all-to-all-done.1 = bf16[16,32,16,128]{3,1,0,2:T(8,128)(2,1)} async-done(((bf16[16,32,16,128]{3,1,0,2:T(8,128)(2,1)}), bf16[16,32,16,128]{3,1,0,2:T(8,128)(2,1)}, u32[]{:S(2)}, u32[]{:S(2)}) %all-to-all-start.1) | async-done | bytes 2097184 | tf_op jit(solution)/shard_map/all_to_all | solution.py:96
  132.7 2.4 copy.19
  135.1 3.9 fusion.17
  140.4 3.5 all-to-all-start.2
  145.3 7.3 %all-to-all-done.2 = bf16[32,32,2,128]{3,2,1,0:T(2,128)(2,1)S(1)} async-done(((bf16[32,32,2,128]{3,2,1,0:T(2,128)(2,1)}), bf16[32,32,2,128]{3,2,1,0:T(2,128)(2,1)S(1)}, u32[]{:S(2)}, u32[]{:S(2)}) %all-to-all-start.2) | async-done | bytes 524320 | tf_op jit(solution)/shard_map/all_to_all | solution.py:102
  152.7 13.9 %all-to-all-start.3 = ((bf16[32,32,2,128]{3,2,1,0:T(2,128)(2,1)}), bf16[32,32,2,128]{3,2,1,0:T(2,128)(2,1)S(1)}, u32[]{:S(2)}, u32[]{:S(2)}) async-start(bf16[32,32,2,128]{3,2,1,0:T(2,128)(2,1)} %copy.22), calls=%async_computation.3 | async-start | bytes 1048576 | tf_op jit(solution)/shard_map/all_to_all | solution.py:105
  166.9 8.1 %all-to-all-done.3 = bf16[32,32,2,128]{3,2,1,0:T(2,128)(2,1)S(1)} async-done(((bf16[32,32,2,128]{3,2,1,0:T(2,128)(2,1)}), bf16[32,32,2,128]{3,2,1,0:T(2,128)(2,1)S(1)}, u32[]{:S(2)}, u32[]{:S(2)}) %all-to-all-start.3) | async-done | bytes 524320 | tf_op jit(solution)/shard_map/all_to_all | solution.py:105
  175.8 8.2 %fusion.37 = f32[8,32,2,1,128]{4,3,2,1,0:T(1,128)S(1)} fusion(bf16[8,32,2,128,128]{4,3,2,1,0:T(8,128)(2,1)} %param.8, bf16[8,32,2,128,1]{3,1,2,0,4:T(8,128)(2,1)S(1)} %get-tuple-element.13), kind=kOutput, calls=%fused_computation.45 | convolution fusion | flops 16777216 | bytes 17170432 | tf_op jit(solution)/shard_map/abcd,abcde->abce/dot_general | solution.py:80
  184.1 8.2 %fusion.39 = f32[8,32,2,1,128]{4,3,2,1,0:T(1,128)S(1)} fusion(bf16[8,32,2,128,128]{4,3,2,1,0:T(8,128)(2,1)} %param.7, bf16[8,32,2,128,1]{3,1,2,0,4:T(8,128)(2,1)S(1)} %get-tuple-element.13), kind=kOutput, calls=%fused_computation.47 | convolution fusion | flops 16777216 | bytes 17170432 | tf_op jit(solution)/shard_map/abcd,abcde->abce/dot_general | solution.py:77
  192.3 4.4 %fusion.33 = f32[8,32,2,1,128]{4,3,2,1,0:T(1,128)S(1)} fusion(bf16[8,32,2,128,128]{4,3,2,1,0:T(8,128)(2,1)S(1)} %bitcast.98, bf16[8,32,2,128,1]{3,1,2,0,4:T(8,128)(2,1)S(1)} %get-tuple-element.14), kind=kOutput, calls=%fused_computation.41 | convolution fusion | flops 16777216 | bytes 17170432 | tf_op jit(solution)/shard_map/abcd,abcde->abce/dot_general | solution.py:82
  197.2 4.4 %fusion.35 = f32[8,32,2,1,128]{4,3,2,1,0:T(1,128)S(1)} fusion(bf16[8,32,2,128,128]{4,3,2,1,0:T(8,128)(2,1)S(1)} %bitcast.100, bf16[8,32,2,128,1]{3,1,2,0,4:T(8,128)(2,1)S(1)} %get-tuple-element.14), kind=kOutput, calls=%fused_computation.43 | convolution fusion | flops 16777216 | bytes 17170432 | tf_op jit(solution)/shard_map/abcd,abcde->abce/dot_general | solution.py:79
  205.1 3.5 all-to-all-start.4
  209.9 7.4 %all-to-all-done.4 = bf16[8,128,2,128]{3,2,0,1:T(2,128)(2,1)S(1)} async-done(((bf16[8,128,2,128]{3,2,0,1:T(2,128)(2,1)}), bf16[8,128,2,128]{3,2,0,1:T(2,128)(2,1)S(1)}, u32[]{:S(2)}, u32[]{:S(2)}) %all-to-all-start.4) | async-done | bytes 524320 | tf_op jit(solution)/shard_map/all_to_all | solution.py:117
  217.4 3.7 all-to-all-start.5
  221.2 8.6 %all-to-all-done.5 = bf16[8,128,2,128]{3,2,0,1:T(2,128)(2,1)S(1)} async-done(((bf16[8,128,2,128]{3,2,0,1:T(2,128)(2,1)}), bf16[8,128,2,128]{3,2,0,1:T(2,128)(2,1)S(1)}, u32[]{:S(2)}, u32[]{:S(2)}) %all-to-all-start.5) | async-done | bytes 524320 | tf_op jit(solution)/shard_map/all_to_all | solution.py:120
  230.0 3.8 convolution_convert_fusion
  235.6 3.5 copy.29
  239.1 3.6 all-to-all-start.6
  242.7 5.1 %copy.31 = bf16[128,32,2,128]{3,2,1,0:T(2,128)(2,1)} copy(bf16[128,32,2,128]{3,0,2,1:T(8,128)(2,1)} %get-tuple-element.6) | data formatting | bytes 4194304 | tf_op jit(solution)/shard_map/slice | solution.py:129
  247.8 43.0 %all-to-all-done.6 = bf16[128,32,2,128]{3,2,1,0:T(2,128)(2,1)S(1)} async-done(((bf16[128,32,2,128]{3,2,1,0:T(2,128)(2,1)}), bf16[128,32,2,128]{3,2,1,0:T(2,128)(2,1)S(1)}, u32[]{:S(2)}, u32[]{:S(2)}) %all-to-all-start.6) | async-done | bytes 2097184 | tf_op jit(solution)/shard_map/all_to_all | solution.py:128
  290.8 4.6 %all-to-all-start.7 = ((bf16[128,32,2,128]{3,2,1,0:T(2,128)(2,1)}), bf16[128,32,2,128]{3,2,1,0:T(2,128)(2,1)}, u32[]{:S(2)}, u32[]{:S(2)}) async-start(bf16[128,32,2,128]{3,2,1,0:T(2,128)(2,1)} %copy.31), calls=%async_computation.7 | async-start | bytes 4194304 | tf_op jit(solution)/shard_map/all_to_all | solution.py:129
  295.6 3.1 copy.30
  298.7 44.5 %all-to-all-done.7 = bf16[128,32,2,128]{3,2,1,0:T(2,128)(2,1)} async-done(((bf16[128,32,2,128]{3,2,1,0:T(2,128)(2,1)}), bf16[128,32,2,128]{3,2,1,0:T(2,128)(2,1)}, u32[]{:S(2)}, u32[]{:S(2)}) %all-to-all-start.7) | async-done | bytes 2097184 | tf_op jit(solution)/shard_map/all_to_all | solution.py:129
  343.2 4.4 %copy.32 = bf16[8,16,32,2,128]{4,3,0,2,1:T(2,128)(2,1)} copy(bf16[8,16,32,2,128]{4,3,2,1,0:T(2,128)(2,1)} %bitcast.40) | data formatting | bytes 4194304 | tf_op jit(solution)/shard_map/all_to_all | solution.py:129
  347.7 24.7 %fusion.13 = f32[256,16,32,128]{3,0,2,1:T(8,128)} fusion(bf16[16,32,16,128]{3,2,1,0:T(8,128)(2,1)} %bitcast.102, bf16[16,32,16,128]{3,2,1,0:T(8,128)(2,1)S(1)} %bitcast.101, bf16[16,256]{1,0:T(8,128)(2,1)S(1)} %get-tuple-element.18, bf16[16,256]{1,0:T(8,128)(2,1)S(1)} %get-tuple-element.17), kind=kOutput, calls=%fused_computation.15 | convolution fusion | flops 1082163200 | bytes 71319552 | tf_op jit(solution)/shard_map/xykc,kz->xyzc/dot_general | solution.py:131
  372.4 46.7 %fusion.7 = bf16[16,32,256,128]{3,2,1,0:T(8,128)(2,1)} fusion(f32[256,16,32,128]{3,0,2,1:T(8,128)} %fusion.13, f32[128]{0:T(128)S(1)} %convert_element_type.130, bf16[16,32,256,128]{3,2,1,0:T(8,128)(2,1)} %param.6, bf16[128,128]{1,0:T(8,128)(2,1)S(1)} %copy-done), kind=kOutput, calls=%fused_computation.8 | convolution fusion | flops 4479516672 | bytes 134251008 | tf_op jit(solution)/shard_map/xyzc,cd->xyzd/dot_general | solution.py:137
  (53 shorter events, 15.8 us)
Async XLA Ops:
  0.0 372.4 %copy-start = (bf16[128,128]{1,0:T(8,128)(2,1)S(1)}, bf16[128,128]{1,0:T(8,128)(2,1)}, u32[]{:S(2)}) copy-start(bf16[128,128]{1,0:T(8,128)(2,1)} %param.10) | copy-start | bytes 98308
  25.0 55.5 %all-to-all-start = ((bf16[16,32,16,128]{3,1,0,2:T(8,128)(2,1)}), bf16[16,32,16,128]{3,1,0,2:T(8,128)(2,1)S(1)}, u32[]{:S(2)}, u32[]{:S(2)}) async-start(bf16[16,32,16,128]{3,1,0,2:T(8,128)(2,1)} %copy.16), calls=%async_computation | async-start | bytes 4194304 | tf_op jit(solution)/shard_map/all_to_all | solution.py:95
  80.5 52.2 %all-to-all-start.1 = ((bf16[16,32,16,128]{3,1,0,2:T(8,128)(2,1)}), bf16[16,32,16,128]{3,1,0,2:T(8,128)(2,1)}, u32[]{:S(2)}, u32[]{:S(2)}) async-start(bf16[16,32,16,128]{3,1,0,2:T(8,128)(2,1)} %copy.18), calls=%async_computation.1 | async-start | bytes 4194304 | tf_op jit(solution)/shard_map/all_to_all | solution.py:96
  87.2 56.7 %copy-start.2 = (s32[8,2]{0,1:T(2,128)S(1)}, s32[8,2]{0,1:T(2,128)}, u32[]{:S(2)}) copy-start(s32[8,2]{0,1:T(2,128)} %param.9) | copy-start | bytes 196
  140.4 12.3 %all-to-all-start.2 = ((bf16[32,32,2,128]{3,2,1,0:T(2,128)(2,1)}), bf16[32,32,2,128]{3,2,1,0:T(2,128)(2,1)S(1)}, u32[]{:S(2)}, u32[]{:S(2)}) async-start(bf16[32,32,2,128]{3,2,1,0:T(2,128)(2,1)} %copy.20), calls=%async_computation.2 | async-start | bytes 1048576 | tf_op jit(solution)/shard_map/all_to_all | solution.py:102
  152.7 22.4 %all-to-all-start.3 = ((bf16[32,32,2,128]{3,2,1,0:T(2,128)(2,1)}), bf16[32,32,2,128]{3,2,1,0:T(2,128)(2,1)S(1)}, u32[]{:S(2)}, u32[]{:S(2)}) async-start(bf16[32,32,2,128]{3,2,1,0:T(2,128)(2,1)} %copy.22), calls=%async_computation.3 | async-start | bytes 1048576 | tf_op jit(solution)/shard_map/all_to_all | solution.py:105
  175.8 16.4 %slice-start = ((s8[16777216]{0:T(1024)(128)(4,1)}), s8[4194304]{0:T(1024)(128)(4,1)S(1)}, s32[]{:S(2)}) async-start(s8[16777216]{0:T(1024)(128)(4,1)} %bitcast.97), calls=%async_computation.8 | async-start | bytes 8388608
  175.8 16.4 %slice-start.1 = ((s8[16777216]{0:T(1024)(128)(4,1)}), s8[4194304]{0:T(1024)(128)(4,1)S(1)}, s32[]{:S(2)}) async-start(s8[16777216]{0:T(1024)(128)(4,1)} %bitcast.97), calls=%async_computation.9 | async-start | bytes 8388608
  184.0 8.2 %slice-start.2 = ((s8[16777216]{0:T(1024)(128)(4,1)}), s8[4194304]{0:T(1024)(128)(4,1)S(1)}, s32[]{:S(2)}) async-start(s8[16777216]{0:T(1024)(128)(4,1)} %bitcast.97), calls=%async_computation.10 | async-start | bytes 8388608
  184.0 8.2 %slice-start.3 = ((s8[16777216]{0:T(1024)(128)(4,1)}), s8[4194304]{0:T(1024)(128)(4,1)S(1)}, s32[]{:S(2)}) async-start(s8[16777216]{0:T(1024)(128)(4,1)} %bitcast.97), calls=%async_computation.11 | async-start | bytes 8388608
  184.0 12.7 %slice-start.4 = ((s8[16777216]{0:T(1024)(128)(4,1)}), s8[4194304]{0:T(1024)(128)(4,1)S(1)}, s32[]{:S(2)}) async-start(s8[16777216]{0:T(1024)(128)(4,1)} %bitcast.99), calls=%async_computation.12 | async-start | bytes 8388608
  184.0 12.7 %slice-start.5 = ((s8[16777216]{0:T(1024)(128)(4,1)}), s8[4194304]{0:T(1024)(128)(4,1)S(1)}, s32[]{:S(2)}) async-start(s8[16777216]{0:T(1024)(128)(4,1)} %bitcast.99), calls=%async_computation.13 | async-start | bytes 8388608
  192.3 4.5 %slice-start.6 = ((s8[16777216]{0:T(1024)(128)(4,1)}), s8[4194304]{0:T(1024)(128)(4,1)S(1)}, s32[]{:S(2)}) async-start(s8[16777216]{0:T(1024)(128)(4,1)} %bitcast.99), calls=%async_computation.14 | async-start | bytes 8388608
  192.3 4.9 %slice-start.7 = ((s8[16777216]{0:T(1024)(128)(4,1)}), s8[4194304]{0:T(1024)(128)(4,1)S(1)}, s32[]{:S(2)}) async-start(s8[16777216]{0:T(1024)(128)(4,1)} %bitcast.99), calls=%async_computation.15 | async-start | bytes 8388608
  205.1 12.3 %all-to-all-start.4 = ((bf16[8,128,2,128]{3,2,0,1:T(2,128)(2,1)}), bf16[8,128,2,128]{3,2,0,1:T(2,128)(2,1)S(1)}, u32[]{:S(2)}, u32[]{:S(2)}) async-start(bf16[8,128,2,128]{3,2,0,1:T(2,128)(2,1)} %copy.25), calls=%async_computation.4 | async-start | bytes 1048576 | tf_op jit(solution)/shard_map/all_to_all | solution.py:117
  217.4 12.5 %all-to-all-start.5 = ((bf16[8,128,2,128]{3,2,0,1:T(2,128)(2,1)}), bf16[8,128,2,128]{3,2,0,1:T(2,128)(2,1)S(1)}, u32[]{:S(2)}, u32[]{:S(2)}) async-start(bf16[8,128,2,128]{3,2,0,1:T(2,128)(2,1)} %copy.27), calls=%async_computation.5 | async-start | bytes 1048576 | tf_op jit(solution)/shard_map/all_to_all | solution.py:120
  235.6 59.9 %copy-start.3 = (bf16[128]{0:T(256)(128)(2,1)S(1)}, bf16[128]{0:T(256)(128)(2,1)}, u32[]{:S(2)}) copy-start(bf16[128]{0:T(256)(128)(2,1)} %param.11) | copy-start | bytes 772
  239.1 51.7 %all-to-all-start.6 = ((bf16[128,32,2,128]{3,2,1,0:T(2,128)(2,1)}), bf16[128,32,2,128]{3,2,1,0:T(2,128)(2,1)S(1)}, u32[]{:S(2)}, u32[]{:S(2)}) async-start(bf16[128,32,2,128]{3,2,1,0:T(2,128)(2,1)} %copy.29), calls=%async_computation.6 | async-start | bytes 4194304 | tf_op jit(solution)/shard_map/all_to_all | solution.py:128
  290.8 4.7 %copy-start.1 = (bf16[128,32,2,128]{3,2,1,0:T(2,128)(2,1)}, bf16[128,32,2,128]{3,2,1,0:T(2,128)(2,1)S(1)}, u32[]{:S(2)}) copy-start(bf16[128,32,2,128]{3,2,1,0:T(2,128)(2,1)S(1)} %all-to-all-done.6) | copy-start | bytes 6291460
  290.8 52.4 %all-to-all-start.7 = ((bf16[128,32,2,128]{3,2,1,0:T(2,128)(2,1)}), bf16[128,32,2,128]{3,2,1,0:T(2,128)(2,1)}, u32[]{:S(2)}, u32[]{:S(2)}) async-start(bf16[128,32,2,128]{3,2,1,0:T(2,128)(2,1)} %copy.31), calls=%async_computation.7 | async-start | bytes 4194304 | tf_op jit(solution)/shard_map/all_to_all | solution.py:129
where the time goes:
time: 423 us; the launch traced here: 419 us
  waiting for transfers between devices  209 us (49%)
  matrix products  125 us (30%)
  starting transfers between devices  44.3 us (10%)
  local copies, waits for them, and re-layouts  39.1 us (9%)
    dot_general x1, matrix products, per_device(): jnp.einsum('xyzc,cd->xyzd', grid_features, local_weight, preferred_elemen...  46.7 us
    all_to_all x1, waiting for transfers between devices, per_device(): lax.all_to_all(depth_imag, 'aa', split_axis=2, concat_axis=0, tiled=True)  45.5 us
    all_to_all x1, waiting for transfers between devices, per_device(): lax.all_to_all(depth_real, 'aa', split_axis=2, concat_axis=0, tiled=True)  44.8 us
    all_to_all x1, waiting for transfers between devices, per_device(): lax.all_to_all(result[NX:], 'aa', split_axis=0, concat_axis=2, tiled=True)  44.5 us
    all_to_all x1, waiting for transfers between devices, per_device(): lax.all_to_all(result[:NX], 'aa', split_axis=0, concat_axis=2, tiled=True)  43 us
    dot_general x1, matrix products, per_device(): jnp.einsum('xykc,kz->xyzc', jnp.concatenate(back_field, axis=2), inverse_...  24.7 us
    dot_general x1, matrix products, per_device(): jnp.einsum('xyzc,zk->xykc', grid_features, forward_depth, preferred_eleme...  18.5 us
    all_to_all x1, starting transfers between devices, per_device(): lax.all_to_all(result[KX:].astype(jnp.bfloat16), 'ba', split_axis=0, conc...  13.9 us
  transfers between devices with their start and end apart: 8, of which 8 were waited for; matrix products, arithmetic and copies ran while one was open for 4% of the time, Pallas kernels for 0%

commit v1 on v0

v1 whole, which is shorter than its diff:
```python
import jax
import jax.numpy as jnp
import numpy as np
from jax import lax
from jax.experimental import pallas as pl
from jax.experimental.pallas import tpu as pltpu
from jax.sharding import PartitionSpec as P

BF = jnp.bfloat16
F32 = jnp.float32
CHUNKS = 2


def kept_modes(length, number):
    pos = np.arange(number)
    return np.where(pos < number // 2, pos, pos + (length - number))


def tables(length, modes):
    steps = (np.arange(length)[:, None] * modes[None, :]) % length
    angles = steps.astype(np.float64) * (2.0 * np.pi / length)
    return np.cos(angles), np.sin(angles)


def block_order(count):
    order = [0]
    bit = count // 2
    while bit:
        order = order + [q + bit for q in order]
        bit //= 2
    return order


def dot(a, b):
    return jnp.dot(a, b, preferred_element_type=F32)


def swap(x, count, bit):
    return lax.ppermute(x, "ba", [(i, i ^ bit) for i in range(count)])


def forward_plane(g, fz, ty, chunk, chunks, na, nb, kz2, kyl):
    Xl, Yl, NZ, C = g.shape
    KZ = kz2 * na
    Xc = Xl // chunks
    half = nb // 2
    rows = 2 * kyl

    def body(g_ref, fz_ref, ty_ref, rest_ref, send_ref, s_ref):
        fzv = fz_ref[...]
        for y in range(0, Yl, 2):
            r = dot(fzv, jnp.concatenate([g_ref[0, y], g_ref[0, y + 1]], axis=1))
            s_ref[pl.ds(y, 2 * KZ, stride=Yl), :] = r[:, :C]
            s_ref[pl.ds(y + 1, 2 * KZ, stride=Yl), :] = r[:, C:]
        tyv = ty_ref[...]
        for k in range(0, KZ, 2):
            lo = s_ref[k * 2 * Yl : (k + 1) * 2 * Yl, :]
            hi = s_ref[(k + 1) * 2 * Yl : (k + 2) * 2 * Yl, :]
            o = dot(tyv, jnp.concatenate([lo, hi], axis=1).astype(BF)).astype(BF)
            for u in range(2):
                a, j = divmod(k + u, kz2)
                for n in range(nb):
                    ref = rest_ref if n < half else send_ref
                    ref[n % half, a, 0, j] = o[n * rows : (n + 1) * rows, u * C : (u + 1) * C]

    shape = (half, na, Xc, kz2, rows, C)
    block = pl.BlockSpec((half, na, 1, kz2, rows, C), lambda x: (0, 0, x, 0, 0, 0))
    out = jax.ShapeDtypeStruct(shape, BF)
    return pl.pallas_call(
        body,
        grid=(Xc,),
        in_specs=[
            pl.BlockSpec((1, Yl, NZ, C), lambda x: (x + chunk * Xc, 0, 0, 0)),
            pl.BlockSpec(fz.shape, lambda x: (0, 0)),
            pl.BlockSpec(ty.shape, lambda x: (0, 0)),
        ],
        out_specs=[block, block],
        out_shape=[out, out],
        scratch_shapes=[pltpu.VMEM((2 * KZ * Yl, C), F32)],
        name="forward_plane",
    )(g, fz, ty)


def forward_first(parts, tx, nb, kxl, kz2, kyl, C):
    KX = kxl * nb
    NX = tx.shape[1] // 2
    R = kz2 * 2 * kyl
    count = len(parts)

    def body(*refs):
        tx_ref = refs[count]
        o_ref, s_ref = refs[count + 1 :]
        size = NX * R // count
        for h in range(count):
            s_ref[h * size : (h + 1) * size, :] = refs[h][...].astype(F32)
        txv = tx_ref[...]
        for j in range(kz2):
            cols = []
            for m in range(kyl):
                parts_ = [
                    s_ref[pl.ds(j * 2 * kyl + ri * kyl + m, NX, stride=R), :] for ri in range(2)
                ]
                cols.append(jnp.concatenate(parts_, axis=0).astype(BF))
            o = dot(txv, jnp.concatenate(cols, axis=1)).astype(BF)
            for n in range(nb):
                for m in range(kyl):
                    o_ref[n, j, m] = o[
                        n * 2 * kxl : (n + 1) * 2 * kxl, m * C : (m + 1) * C
                    ]

    return pl.pallas_call(
        body,
        out_shape=jax.ShapeDtypeStruct((nb, kz2, kyl, 2 * kxl, C), BF),
        scratch_shapes=[pltpu.VMEM((NX * R, C), F32)],
        name="forward_first",
    )(*[p.reshape(-1, C) for p in parts], tx)


def mix(spec, wr, wi, keep):
    nb, kz2, kyl, rows, C = spec.shape
    kxl, KY = wr.shape[:2]
    kyc = min(4, kyl)
    steps = kyl // kyc
    levels = jnp.broadcast_to(keep.T[:, :, None], (kz2, kxl, C))

    def body(s_ref, wr_ref, wi_ref, keep_ref, o_ref):
        base = pl.program_id(1) * kyc
        row = lax.broadcasted_iota(jnp.int32, (rows, 2 * C), 0)
        row = jnp.where(row >= kxl, row - kxl, row)
        kept = keep_ref[0]
        for t in range(kyc):
            ky = base + t
            level = jnp.where(ky < KY // 2, ky, KY - 1 - ky)
            s = s_ref[0, 0, t]
            acc = None
            for i in range(kxl):
                w = jnp.concatenate([wr_ref[i, t, 0], wi_ref[i, t, 0]], axis=1)
                res = dot(s, w)
                acc = res if acc is None else jnp.where(row == i, res, acc)
            re = acc[:kxl, :C] - acc[kxl:, C:]
            im = acc[:kxl, C:] + acc[kxl:, :C]
            on = level < kept
            re = jnp.where(on, re, 0.0)
            im = jnp.where(on, im, 0.0)
            o_ref[0, 0, t] = jnp.concatenate([re, im], axis=0).astype(BF)

    sblock = pl.BlockSpec((1, 1, kyc, rows, C), lambda j, s: (s // steps, j, s % steps, 0, 0))
    wblock = pl.BlockSpec((kxl, kyc, 1, C, C), lambda j, s: (0, s, j, 0, 0))
    return pl.pallas_call(
        body,
        grid=(kz2, nb * steps),
        in_specs=[sblock, wblock, wblock, pl.BlockSpec((1, kxl, C), lambda j, s: (j, 0, 0))],
        out_specs=sblock,
        out_shape=jax.ShapeDtypeStruct(spec.shape, BF),
        name="mix",
    )(spec, wr, wi, levels)


def inverse_first(mixed, txi, chunks, na):
    nb, kz2, kyl, rows, C = mixed.shape
    NX = txi.shape[0] // 2
    R = kz2 * 2 * kyl
    size = NX * R // chunks

    def body(m_ref, tx_ref, *rest):
        outs, s_ref = rest[:chunks], rest[chunks]
        txv = tx_ref[...]
        for j in range(kz2):
            cols = [
                jnp.concatenate([m_ref[n, j, m] for n in range(nb)], axis=0) for m in range(kyl)
            ]
            o = dot(txv, jnp.concatenate(cols, axis=1))
            for ri in range(2):
                for m in range(kyl):
                    s_ref[pl.ds(j * 2 * kyl + ri * kyl + m, NX, stride=R), :] = o[
                        ri * NX : (ri + 1) * NX, m * C : (m + 1) * C
                    ]
        for h in range(chunks):
            outs[h][...] = s_ref[h * size : (h + 1) * size, :].astype(BF)

    outs = pl.pallas_call(
        body,
        out_shape=[jax.ShapeDtypeStruct((size, C), BF)] * chunks,
        scratch_shapes=[pltpu.VMEM((NX * R, C), F32)],
        name="inverse_first",
    )(mixed, txi)
    Xc = NX // na // chunks
    return [o.reshape(na, Xc, kz2, 2 * kyl, C) for o in outs]


def finish(g, pieces, uy, iz, lw2, lb2, prior, chunk, chunks):
    Xl, Yl, NZ, C = g.shape
    na, Xc, kz2, rows, _ = pieces[0].shape
    KZ = na * kz2
    nb = len(pieces)

    def body(*refs):
        g_ref, uy_ref, iz_ref, lw_ref, lb_ref = refs[:5]
        p_refs = refs[5 : 5 + nb]
        o_ref, s_ref = refs[-2:]
        uyv = uy_ref[...]
        for k in range(0, KZ, 2):
            cols = []
            for u in range(2):
                a, j = divmod(k + u, kz2)
                cols.append(jnp.concatenate([p[a, 0, j] for p in p_refs], axis=0))
            o = dot(uyv, jnp.concatenate(cols, axis=1))
            for u in range(2):
                for ri in range(2):
                    s_ref[pl.ds((k + u) * 2 + ri, Yl, stride=2 * KZ), :] = o[
                        ri * Yl : (ri + 1) * Yl, u * C : (u + 1) * C
                    ]

        lwv = lw_ref[...]
        izv = iz_ref[...]
        lbv = lb_ref[...]

        def step(t, carry):
            y = t * 2
            lo = s_ref[pl.ds(pl.multiple_of(y * 2 * KZ, 2 * KZ), 2 * KZ), :]
            hi = s_ref[pl.ds(pl.multiple_of((y + 1) * 2 * KZ, 2 * KZ), 2 * KZ), :]
            b = jnp.concatenate([lo, hi], axis=1).astype(BF)
            cells = jnp.concatenate([g_ref[0, y], g_ref[0, y + 1], izv], axis=1)
            maps = jnp.concatenate([lwv, b, lbv], axis=0)
            v = dot(cells, maps).astype(BF)
            inner = v * (BF(0.7978845608028654) + BF(0.035677408136300125) * (v * v))
            half = BF(0.5) * v
            r = half + half * jnp.tanh(inner)
            o_ref[0, y] = r[:, :C]
            o_ref[0, y + 1] = r[:, C:]
            return carry

        lax.fori_loop(0, Yl // 2, step, 0, unroll=4)

    whole = lambda a: pl.BlockSpec(a.shape, lambda x: (0,) * a.ndim)
    cell = pl.BlockSpec((1, Yl, NZ, C), lambda x: (x + chunk * Xc, 0, 0, 0))
    piece = pl.BlockSpec((na, 1, kz2, rows, C), lambda x: (0, x, 0, 0, 0))
    args = [g, uy, iz, lw2, lb2, *pieces]
    specs = [cell, whole(uy), whole(iz), whole(lw2), whole(lb2)] + [piece] * nb
    aliases = {}
    if prior is not None:
        aliases = {len(args): 0}
        args.append(prior)
        specs.append(pl.BlockSpec(memory_space=pl.ANY))
    return pl.pallas_call(
        body,
        grid=(Xc,),
        in_specs=specs,
        out_specs=cell,
        out_shape=jax.ShapeDtypeStruct(g.shape, BF),
        scratch_shapes=[pltpu.VMEM((2 * KZ * Yl, C), F32)],
        input_output_aliases=aliases,
        name="finish",
    )(*args)


def stack_forward(cos, sin):
    return np.block([[cos.T, sin.T], [-sin.T, cos.T]])


def solution(mesh):
    na, nb = mesh.shape["aa"], mesh.shape["ba"]

    def per_device(g, wr, wi, keep, lw, lb):
        Xl, Yl, NZ, C = g.shape
        kxl, KY, kz2 = wr.shape[:3]
        NX, NY, KX, KZ, kyl = Xl * na, Yl * nb, kxl * nb, kz2 * na, KY // nb
        chunks = CHUNKS
        Xc = Xl // chunks
        order = block_order(nb)

        cz, sz = tables(NZ, np.arange(KZ))
        fz = np.stack([cz.T, -sz.T], axis=1).reshape(2 * KZ, NZ).astype(BF)
        factor = np.where(np.arange(KZ) == 0, 1.0, 2.0) / (NX * NY * NZ)
        iz = np.stack([cz * factor, -sz * factor], axis=2).reshape(NZ, 2 * KZ).astype(BF)

        cy, sy = tables(NY, kept_modes(NY, KY))
        ty_all, uy_all = [], []
        for b in range(nb):
            rows = slice(b * Yl, (b + 1) * Yl)
            ty, uy = [], []
            for q in order:
                cols = slice((b ^ q) * kyl, ((b ^ q) + 1) * kyl)
                c, s = cy[rows, cols], sy[rows, cols]
                ty.append(np.block([[c.T, s.T], [-s.T, c.T]]))
                uy.append(np.block([[c, -s], [s, c]]))
            ty_all.append(np.concatenate(ty, axis=0))
            uy_all.append(np.concatenate(uy, axis=1))
        me = lax.axis_index("ba")
        ty = lax.dynamic_index_in_dim(jnp.asarray(np.stack(ty_all).astype(BF)), me, 0, False)
        uy = lax.dynamic_index_in_dim(jnp.asarray(np.stack(uy_all).astype(BF)), me, 0, False)

        cx, sx = tables(NX, kept_modes(NX, KX))
        places = np.arange(NX).reshape(na, chunks, Xc).transpose(1, 0, 2).reshape(-1)
        cx, sx = cx[places], sx[places]
        tx, txi = [], []
        for n in range(nb):
            c, s = cx[:, n * kxl : (n + 1) * kxl], sx[:, n * kxl : (n + 1) * kxl]
            tx.append(np.block([[c.T, s.T], [-s.T, c.T]]))
            txi.append(np.block([[c, -s], [s, c]]))
        tx = jnp.asarray(np.concatenate(tx, axis=0).astype(BF))
        txi = jnp.asarray(np.concatenate(txi, axis=1).astype(BF))

        parts = []
        for h in range(chunks):
            rest, send = forward_plane(g, jnp.asarray(fz), ty, h, chunks, na, nb, kz2, kyl)
            bit = 1
            while True:
                got = swap(send, nb, bit)
                rest = (rest.astype(F32) + got.astype(F32)).astype(BF)
                bit *= 2
                if bit == nb:
                    break
                mid = rest.shape[0] // 2
                rest, send = rest[:mid], rest[mid:]
            parts.append(lax.all_to_all(rest[0], "aa", 0, 0, tiled=True))
        spec = forward_first(parts, tx, nb, kxl, kz2, kyl, C)
        spec = lax.all_to_all(spec, "ba", 0, 0, tiled=True)
        mixed = mix(spec, wr, wi, keep)
        mixed = lax.all_to_all(mixed, "ba", 0, 0, tiled=True)
        backs = inverse_first(mixed, txi, chunks, na)

        zero = jnp.zeros_like(lw)
        lw2 = jnp.concatenate(
            [jnp.concatenate([lw, zero], axis=1), jnp.concatenate([zero, lw], axis=1)], axis=0
        )
        lb2 = jnp.pad(jnp.tile(lb, 2)[None, :], ((0, 15), (0, 0)))
        iz = np.concatenate([iz, np.ones((NZ, 1)), np.zeros((NZ, 15))], axis=1).astype(BF)
        out = None
        for h in range(chunks):
            pieces = [lax.all_to_all(backs[h], "aa", 0, 0, tiled=True)]
            bit = nb // 2
            while bit:
                pieces = pieces + [swap(p, nb, bit) for p in pieces]
                bit //= 2
            out = finish(g, pieces, uy, jnp.asarray(iz), lw2, lb2, out, h, chunks)
        return out

    in_specs = (
        P("aa", "ba", None, None),
        P("ba", None, "aa", None, None),
        P("ba", None, "aa", None, None),
        P("ba", "aa"),
        P(),
        P(),
    )
    return jax.shard_map(
        per_device,
        mesh=mesh,
        in_specs=in_specs,
        out_specs=P("aa", "ba", None, None),
        check_vma=False,
    )
```

time: 423 us -> 226 us (0.53)
  waiting for transfers between devices: 209 us -> 48.1 us
  matrix products: 125 us -> 0 us
  Pallas kernels: 0 us -> 93.7 us
  blocking collectives: 0 us -> 55.9 us
  local copies, waits for them, and re-layouts: 39.1 us -> 5.68 us
  starting transfers between devices: 44.3 us -> 17.1 us
    all_to_all x8 -> x2, waiting for transfers between devices: 209 us -> 13.9 us  [the longest x1 13.3 us: per_device(): pieces = [lax.all_to_all(backs[h], 'aa', 0, 0, tiled=True)]]
    dot_general x11 -> x0, matrix products: 125 us -> none  [the longest x1 46.7 us: per_device(): jnp.einsum('xyzc,cd->xyzd', grid_features, local_weight, preferred_elemen...]
    pallas_call x0 -> x7, Pallas kernels: none -> 93.7 us  [the longest x2 45.2 us: finish(): pl.pallas_call(body, grid=(Xc,), in_specs=specs, out_specs=cell, out_shap...]
    all_to_all x0 -> x4, blocking collectives: none -> 55.9 us  [the longest x1 17.8 us: per_device(): pieces = [lax.all_to_all(backs[h], 'aa', 0, 0, tiled=True)]]
    all_to_all x8 -> x2, starting transfers between devices: 44.3 us -> 9.66 us  [the longest x1 6.03 us: per_device(): parts.append(lax.all_to_all(rest[0], 'aa', 0, 0, tiled=True))]
    ppermute x0 -> x10, waiting for transfers between devices: none -> 34.3 us  [swap(): return lax.ppermute(x, 'ba', [(i, i ^ bit) for i in range(count)])]
    slice x13 -> x2, local copies, waits for them, and re-layouts: 25.9 us -> 0.09 us  [per_device(): rest, send = (rest[:mid], rest[mid:])]
    all_to_all x4 -> x0, local copies, waits for them, and re-layouts: 12.1 us -> none  [the longest x1 4.45 us: per_device(): lax.all_to_all(result[NX:], 'aa', split_axis=0, concat_axis=2, tiled=True)]
  transfers between devices with their start and end apart: 8 -> 12, of which waited for: 8 -> 5; matrix products, arithmetic and copies ran while one was open for 4% -> 3% of each run, Pallas kernels for 0% -> 15%
where the time goes in v1:
time: 226 us; the launch traced here: 224 us
  Pallas kernels  93.7 us (41%)
  blocking collectives  55.9 us (25%)
  waiting for transfers between devices  48.1 us (21%)
  starting transfers between devices  17.1 us (8%)
  local copies, waits for them, and re-layouts  5.68 us (3%)
  other arithmetic  3.64 us (2%)
    pallas_call x2, Pallas kernels, finish(): pl.pallas_call(body, grid=(Xc,), in_specs=specs, out_specs=cell, out_shap...  45.2 us
    ppermute x10, waiting for transfers between devices, swap(): return lax.ppermute(x, 'ba', [(i, i ^ bit) for i in range(count)])  34.3 us
    pallas_call x2, Pallas kernels, forward_plane(): pl.pallas_call(body, grid=(Xc,), in_specs=[pl.BlockSpec((1, Yl, NZ, C), l...  23.5 us
    pallas_call x1, Pallas kernels, mix(): pl.pallas_call(body, grid=(kz2, nb * steps), in_specs=[sblock, wblock, wb...  18.2 us
    all_to_all x1, blocking collectives, per_device(): pieces = [lax.all_to_all(backs[h], 'aa', 0, 0, tiled=True)]  17.8 us
    all_to_all x1, blocking collectives, per_device(): parts.append(lax.all_to_all(rest[0], 'aa', 0, 0, tiled=True))  17.7 us
    all_to_all x1, waiting for transfers between devices, per_device(): pieces = [lax.all_to_all(backs[h], 'aa', 0, 0, tiled=True)]  13.3 us
    all_to_all x1, blocking collectives, per_device(): mixed = lax.all_to_all(mixed, 'ba', 0, 0, tiled=True)  10.2 us
  transfers between devices with their start and end apart: 12, of which 5 were waited for; matrix products, arithmetic and copies ran while one was open for 3% of the time, Pallas kernels for 15%

profile of v1, /device:TPU:0, one launch (start us, length us, event | category | flops | bytes accessed | tf_op | source)
XLA Modules:
  0.0 224.3 jit_solution(7947622915383538297)
XLA Ops:
  0.0 1.3 dynamic-slice_bitcast_fusion.ty_ref
  1.3 11.8 %forward_plane.3 = (bf16[2,8,8,2,16,128]{5,4,3,2,1,0:T(8,128)(2,1)}, bf16[2,8,8,2,16,128]{5,4,3,2,1,0:T(8,128)(2,1)}) custom-call(bf16[16,32,256,128]{3,2,1,0:T(8,128)(2,1)} %refs_0_.3, bf16[32,256]{1,0:T(8,128)(2,1)} %constant.32.clone.fz_ref, bf16[64,64]{1,0:T(8,128)(2,1)} %dynamic-slice_bitcast_fusion.ty_ref), custom_call_target="tpu_custom_call" | custom-call | tf_op jit(solution)/shard_map/forward_plane/pallas_call | solution.py:69
  13.6 11.7 %forward_plane.2 = (bf16[2,8,8,2,16,128]{5,4,3,2,1,0:T(8,128)(2,1)}, bf16[2,8,8,2,16,128]{5,4,3,2,1,0:T(8,128)(2,1)}) custom-call(bf16[16,32,256,128]{3,2,1,0:T(8,128)(2,1)} %refs_0_.3, bf16[32,256]{1,0:T(8,128)(2,1)} %constant.32.clone.fz_ref, bf16[64,64]{1,0:T(8,128)(2,1)} %dynamic-slice_bitcast_fusion.ty_ref), custom_call_target="tpu_custom_call" | custom-call | tf_op jit(solution)/shard_map/forward_plane/pallas_call | solution.py:69
  25.5 1.6 add_convert_fusion
  27.1 3.0 %collective-permute-start.3 = (bf16[1,8,8,2,16,128]{5,4,3,2,1,0:T(8,128)(2,1)S(1)}, bf16[1,8,8,2,16,128]{5,4,3,2,1,0:T(8,128)(2,1)S(1)}, u32[]{:S(2)}, u32[]{:S(2)}) collective-permute-start(bf16[1,8,8,2,16,128]{5,4,3,2,1,0:T(8,128)(2,1)S(1)} %slice.19), channel_id=1, source_target_pairs={{0,2},{1,3},{2,0},{3,1},{4,6},{5,7},{6,4},{7,5},{8,10},{9,11},{10,... | collective-permute-start | bytes 1572872 | tf_op jit(solution)/shard_map/ppermute | solution.py:39
  30.1 12.2 %collective-permute-done.3 = bf16[1,8,8,2,16,128]{5,4,3,2,1,0:T(8,128)(2,1)S(1)} collective-permute-done((bf16[1,8,8,2,16,128]{5,4,3,2,1,0:T(8,128)(2,1)S(1)}, bf16[1,8,8,2,16,128]{5,4,3,2,1,0:T(8,128)(2,1)S(1)}, u32[]{:S(2)}, u32[]{:S(2)}) %collective-permute-start.3) | collective-permute-done | bytes 524320 | tf_op jit(solution)/shard_map/ppermute | solution.py:39
  42.3 0.9 fusion.1
  43.2 6.0 %all-to-all-start.1 = ((bf16[8,8,2,16,128]{4,3,2,1,0:T(8,128)(2,1)}), bf16[8,8,2,16,128]{4,3,2,1,0:T(8,128)(2,1)S(1)}, u32[]{:S(2)}, u32[]{:S(2)}) async-start(bf16[8,8,2,16,128]{4,3,2,1,0:T(8,128)(2,1)} %fusion.1), calls=%async_computation.1 | async-start | bytes 1048576 | tf_op jit(solution)/shard_map/all_to_all | solution.py:316
  49.7 1.6 collective-permute-start.1
  51.2 11.3 %collective-permute-done.1 = bf16[1,8,8,2,16,128]{5,4,3,2,1,0:T(8,128)(2,1)S(1)} collective-permute-done((bf16[1,8,8,2,16,128]{5,4,3,2,1,0:T(8,128)(2,1)S(1)}, bf16[1,8,8,2,16,128]{5,4,3,2,1,0:T(8,128)(2,1)S(1)}, u32[]{:S(2)}, u32[]{:S(2)}) %collective-permute-start.1) | collective-permute-done | bytes 524320 | tf_op jit(solution)/shard_map/ppermute | solution.py:39
  62.7 0.6 all-to-all-done.1
  63.2 17.7 %all_to_all.30 = bf16[8,8,2,16,128]{4,3,2,1,0:T(8,128)(2,1)} all-to-all(bf16[8,8,2,16,128]{4,3,2,1,0:T(8,128)(2,1)S(1)} %fusion), channel_id=1, replica_groups=mesh['aa'=8,'ba'=4] {'aa'}, dimensions={0} | all-to-all | bytes 1048576 | tf_op jit(solution)/shard_map/all_to_all | solution.py:316
  81.0 3.4 %forward_first.1 = bf16[4,2,8,16,128]{4,3,2,1,0:T(8,128)(2,1)} custom-call(bf16[2048,128]{1,0:T(8,128)(2,1)} %bitcast.20, bf16[2048,128]{1,0:T(8,128)(2,1)} %bitcast.19, bf16[64,256]{1,0:T(8,128)(2,1)} %constant.30.clone.refs_2_), custom_call_target="tpu_custom_call" | custom-call | tf_op jit(solution)/shard_map/forward_first/pallas_call | solution.py:111
  84.3 10.1 %all_to_all.31.s_ref = bf16[4,2,8,16,128]{4,3,2,1,0:T(8,128)(2,1)} all-to-all(bf16[4,2,8,16,128]{4,3,2,1,0:T(8,128)(2,1)} %forward_first.1), channel_id=1, replica_groups=mesh['aa'=8,'ba'=4] {'ba'}, dimensions={0} | all-to-all | bytes 524288 | tf_op jit(solution)/shard_map/all_to_all | solution.py:318
  94.4 0.7 broadcast_in_dim.2.keep_ref
  95.1 18.2 %mix.1 = bf16[4,2,8,16,128]{4,3,2,1,0:T(8,128)(2,1)} custom-call(bf16[4,2,8,16,128]{4,3,2,1,0:T(8,128)(2,1)} %all_to_all.31.s_ref, bf16[8,32,2,128,128]{4,3,2,1,0:T(8,128)(2,1)} %wr_ref.1, bf16[8,32,2,128,128]{4,3,2,1,0:T(8,128)(2,1)} %wi_ref.1, s32[2,8,128]{2,1,0:T(8,128)} %broadcast_in_dim.2.keep_ref), custom_call_target="tpu_custom_call" | custom-call | tf_op jit(solution)/shard_map/mix/pallas_call | solution.py:149
  113.2 10.2 %all_to_all.32.m_ref = bf16[4,2,8,16,128]{4,3,2,1,0:T(8,128)(2,1)} all-to-all(bf16[4,2,8,16,128]{4,3,2,1,0:T(8,128)(2,1)} %mix.1), channel_id=1, replica_groups=mesh['aa'=8,'ba'=4] {'ba'}, dimensions={0} | all-to-all | bytes 524288 | tf_op jit(solution)/shard_map/all_to_all | solution.py:320
  123.5 3.4 %inverse_first.1 = (bf16[2048,128]{1,0:T(8,128)(2,1)}, bf16[2048,128]{1,0:T(8,128)(2,1)}) custom-call(bf16[4,2,8,16,128]{4,3,2,1,0:T(8,128)(2,1)} %all_to_all.32.m_ref, bf16[256,64]{1,0:T(8,128)(2,1)} %constant.31.clone.tx_ref), custom_call_target="tpu_custom_call" | custom-call | tf_op jit(solution)/shard_map/inverse_first/pallas_call | solution.py:181
  126.9 17.8 %all_to_all.33.refs_5_ = bf16[8,8,2,16,128]{4,3,2,1,0:T(8,128)(2,1)S(1)} all-to-all(bf16[8,8,2,16,128]{4,3,2,1,0:T(8,128)(2,1)} %bitcast.22), channel_id=1, replica_groups=mesh['aa'=8,'ba'=4] {'aa'}, dimensions={0} | all-to-all | bytes 1048576 | tf_op jit(solution)/shard_map/all_to_all | solution.py:331
  144.7 3.6 %all-to-all-start.4 = ((bf16[8,8,2,16,128]{4,3,2,1,0:T(8,128)(2,1)}), bf16[8,8,2,16,128]{4,3,2,1,0:T(8,128)(2,1)S(1)}, u32[]{:S(2)}, u32[]{:S(2)}) async-start(bf16[8,8,2,16,128]{4,3,2,1,0:T(8,128)(2,1)} %bitcast.21), calls=%async_computation.4 | async-start | bytes 1048576 | tf_op jit(solution)/shard_map/all_to_all | solution.py:331
  148.3 0.8 collective-permute-start.7
  149.2 13.3 %all-to-all-done.4.refs_5_ = bf16[8,8,2,16,128]{4,3,2,1,0:T(8,128)(2,1)S(1)} async-done(((bf16[8,8,2,16,128]{4,3,2,1,0:T(8,128)(2,1)}), bf16[8,8,2,16,128]{4,3,2,1,0:T(8,128)(2,1)S(1)}, u32[]{:S(2)}, u32[]{:S(2)}) %all-to-all-start.4) | async-done | bytes 524320 | tf_op jit(solution)/shard_map/all_to_all | solution.py:331
  162.5 0.9 collective-permute-start.4
  163.4 0.5 collective-permute-start.9
  163.9 10.8 %collective-permute-done.4.refs_6_ = bf16[8,8,2,16,128]{4,3,2,1,0:T(8,128)(2,1)S(1)} collective-permute-done((bf16[8,8,2,16,128]{4,3,2,1,0:T(8,128)(2,1)S(1)}, bf16[8,8,2,16,128]{4,3,2,1,0:T(8,128)(2,1)S(1)}, u32[]{:S(2)}, u32[]{:S(2)}) %collective-permute-start.4) | collective-permute-done | bytes 524320 | tf_op jit(solution)/shard_map/ppermute | solution.py:39
  174.7 0.7 pad.6.refs_4_
  175.4 1.3 dynamic-slice_bitcast_fusion.1.refs_1_
  176.7 0.7 fusion.4.refs_3_
  177.4 0.8 copy-done.10
  178.2 22.6 %finish.2.refs_9_ = bf16[16,32,256,128]{3,2,1,0:T(8,128)(2,1)} custom-call(bf16[16,32,256,128]{3,2,1,0:T(8,128)(2,1)} %refs_0_.3, bf16[64,64]{1,0:T(8,128)(2,1)} %dynamic-slice_bitcast_fusion.1.refs_1_, bf16[256,48]{1,0:T(8,128)(2,1)} %constant.33.clone.refs_2_, bf16[256,256]{1,0:T(8,128)(2,1)} %fusion.4.refs_3_, bf16[16,256]{1,0:T(8,128)(2,1)} %pad.6.refs_4_, ...), custom_call_target="tpu_custom_call" | custom-call | tf_op jit(solution)/shard_map/finish/pallas_call | solution.py:245
  200.8 0.8 copy-done.9
  201.6 22.7 %finish.3 = bf16[16,32,256,128]{3,2,1,0:T(8,128)(2,1)} custom-call(bf16[16,32,256,128]{3,2,1,0:T(8,128)(2,1)} %refs_0_.3, bf16[64,64]{1,0:T(8,128)(2,1)} %dynamic-slice_bitcast_fusion.1.refs_1_, bf16[256,48]{1,0:T(8,128)(2,1)} %constant.33.clone.refs_2_, bf16[256,256]{1,0:T(8,128)(2,1)} %fusion.4.refs_3_, ...), custom_call_target="tpu_custom_call", output_to_operand_aliasing={{}: (9, {})} | custom-call | tf_op jit(solution)/shard_map/finish/pallas_call | solution.py:245
  (42 shorter events, 1.3 us)
Async XLA Ops:
  0.0 174.7 %copy-start = (bf16[128]{0:T(256)(128)(2,1)S(1)}, bf16[128]{0:T(256)(128)(2,1)}, u32[]{:S(2)}) copy-start(bf16[128]{0:T(256)(128)(2,1)} %param.17) | copy-start | bytes 772
  13.1 12.4 %copy-start.6 = (bf16[2,8,8,2,16,128]{5,4,3,2,1,0:T(8,128)(2,1)S(1)}, bf16[2,8,8,2,16,128]{5,4,3,2,1,0:T(8,128)(2,1)}, u32[]{:S(2)}) copy-start(bf16[2,8,8,2,16,128]{5,4,3,2,1,0:T(8,128)(2,1)} %get-tuple-element.13) | copy-start | bytes 3145732
  13.1 12.4 %collective-permute-start.2 = (bf16[2,8,8,2,16,128]{5,4,3,2,1,0:T(8,128)(2,1)}, bf16[2,8,8,2,16,128]{5,4,3,2,1,0:T(8,128)(2,1)}, u32[]{:S(2)}, u32[]{:S(2)}) collective-permute-start(bf16[2,8,8,2,16,128]{5,4,3,2,1,0:T(8,128)(2,1)} %get-tuple-element.14), channel_id=1, source_target_pairs={{0,1},{1,0},{2,3},{3,2},{4,5},{5,4},{6,7},{7,6},{8,9},{9,8},{10,11... | collective-permute-start | bytes 3145736 | tf_op jit(solution)/shard_map/ppermute | solution.py:39
  25.4 23.9 %collective-permute-start = (bf16[2,8,8,2,16,128]{5,4,3,2,1,0:T(8,128)(2,1)}, bf16[2,8,8,2,16,128]{5,4,3,2,1,0:T(8,128)(2,1)S(1)}, u32[]{:S(2)}, u32[]{:S(2)}) collective-permute-start(bf16[2,8,8,2,16,128]{5,4,3,2,1,0:T(8,128)(2,1)} %get-tuple-element.12), channel_id=1, source_target_pairs={{0,1},{1,0},{2,3},{3,2},{4,5},{5,4},{6,7},{7,6},{8,9},{9,8},{10,11... | collective-permute-start | bytes 3145736 | tf_op jit(solution)/shard_map/ppermute | solution.py:39
  27.1 22.2 %copy-start.5 = (bf16[2,8,8,2,16,128]{5,4,3,2,1,0:T(8,128)(2,1)S(1)}, bf16[2,8,8,2,16,128]{5,4,3,2,1,0:T(8,128)(2,1)}, u32[]{:S(2)}) copy-start(bf16[2,8,8,2,16,128]{5,4,3,2,1,0:T(8,128)(2,1)} %get-tuple-element.11) | copy-start | bytes 3145732
  27.1 15.2 %collective-permute-start.3 = (bf16[1,8,8,2,16,128]{5,4,3,2,1,0:T(8,128)(2,1)S(1)}, bf16[1,8,8,2,16,128]{5,4,3,2,1,0:T(8,128)(2,1)S(1)}, u32[]{:S(2)}, u32[]{:S(2)}) collective-permute-start(bf16[1,8,8,2,16,128]{5,4,3,2,1,0:T(8,128)(2,1)S(1)} %slice.19), channel_id=1, source_target_pairs={{0,2},{1,3},{2,0},{3,1},{4,6},{5,7},{6,4},{7,5},{8,10},{9,11},{10,... | collective-permute-start | bytes 1572872 | tf_op jit(solution)/shard_map/ppermute | solution.py:39
  43.2 20.0 %all-to-all-start.1 = ((bf16[8,8,2,16,128]{4,3,2,1,0:T(8,128)(2,1)}), bf16[8,8,2,16,128]{4,3,2,1,0:T(8,128)(2,1)S(1)}, u32[]{:S(2)}, u32[]{:S(2)}) async-start(bf16[8,8,2,16,128]{4,3,2,1,0:T(8,128)(2,1)} %fusion.1), calls=%async_computation.1 | async-start | bytes 1048576 | tf_op jit(solution)/shard_map/all_to_all | solution.py:316
  49.6 44.8 %copy-start.12 = (s32[8,2]{0,1:T(2,128)S(1)}, s32[8,2]{0,1:T(2,128)}, u32[]{:S(2)}) copy-start(s32[8,2]{0,1:T(2,128)} %param.15) | copy-start | bytes 196
  49.7 12.9 %collective-permute-start.1 = (bf16[1,8,8,2,16,128]{5,4,3,2,1,0:T(8,128)(2,1)S(1)}, bf16[1,8,8,2,16,128]{5,4,3,2,1,0:T(8,128)(2,1)S(1)}, u32[]{:S(2)}, u32[]{:S(2)}) collective-permute-start(bf16[1,8,8,2,16,128]{5,4,3,2,1,0:T(8,128)(2,1)S(1)} %slice.17), channel_id=1, source_target_pairs={{0,2},{1,3},{2,0},{3,1},{4,6},{5,7},{6,4},{7,5},{8,10},{9,11},{10,... | collective-permute-start | bytes 1572872 | tf_op jit(solution)/shard_map/ppermute | solution.py:39
  63.2 17.7 %copy-start.4 = (bf16[8,8,2,16,128]{4,3,2,1,0:T(8,128)(2,1)}, bf16[8,8,2,16,128]{4,3,2,1,0:T(8,128)(2,1)S(1)}, u32[]{:S(2)}) copy-start(bf16[8,8,2,16,128]{4,3,2,1,0:T(8,128)(2,1)S(1)} %all-to-all-done.1) | copy-start | bytes 1572868
  113.2 63.5 %copy-start.11 = (bf16[128,128]{1,0:T(8,128)(2,1)S(1)}, bf16[128,128]{1,0:T(8,128)(2,1)}, u32[]{:S(2)}) copy-start(bf16[128,128]{1,0:T(8,128)(2,1)} %param.16) | copy-start | bytes 98308
  144.7 32.7 %copy-start.3 = (bf16[8,8,2,16,128]{4,3,2,1,0:T(8,128)(2,1)}, bf16[8,8,2,16,128]{4,3,2,1,0:T(8,128)(2,1)S(1)}, u32[]{:S(2)}) copy-start(bf16[8,8,2,16,128]{4,3,2,1,0:T(8,128)(2,1)S(1)} %all_to_all.33.refs_5_) | copy-start | bytes 1572868
  144.7 17.8 %all-to-all-start.4 = ((bf16[8,8,2,16,128]{4,3,2,1,0:T(8,128)(2,1)}), bf16[8,8,2,16,128]{4,3,2,1,0:T(8,128)(2,1)S(1)}, u32[]{:S(2)}, u32[]{:S(2)}) async-start(bf16[8,8,2,16,128]{4,3,2,1,0:T(8,128)(2,1)} %bitcast.21), calls=%async_computation.4 | async-start | bytes 1048576 | tf_op jit(solution)/shard_map/all_to_all | solution.py:331
  148.3 15.0 %collective-permute-start.7 = (bf16[8,8,2,16,128]{4,3,2,1,0:T(8,128)(2,1)S(1)}, bf16[8,8,2,16,128]{4,3,2,1,0:T(8,128)(2,1)S(1)}, u32[]{:S(2)}, u32[]{:S(2)}) collective-permute-start(bf16[8,8,2,16,128]{4,3,2,1,0:T(8,128)(2,1)S(1)} %all_to_all.33.refs_5_), channel_id=1, source_target_pairs={{0,2},{1,3},{2,0},{3,1},{4,6},{5,7},{6,4},{7,5},{8,10},{9,11},{10,... | collective-permute-start | bytes 1572872 | tf_op jit(solution)/shard_map/ppermute | solution.py:39
  162.5 38.3 %copy-start.2 = (bf16[8,8,2,16,128]{4,3,2,1,0:T(8,128)(2,1)}, bf16[8,8,2,16,128]{4,3,2,1,0:T(8,128)(2,1)S(1)}, u32[]{:S(2)}) copy-start(bf16[8,8,2,16,128]{4,3,2,1,0:T(8,128)(2,1)S(1)} %all-to-all-done.4.refs_5_) | copy-start | bytes 1572868
  162.5 12.2 %collective-permute-start.4 = (bf16[8,8,2,16,128]{4,3,2,1,0:T(8,128)(2,1)S(1)}, bf16[8,8,2,16,128]{4,3,2,1,0:T(8,128)(2,1)S(1)}, u32[]{:S(2)}, u32[]{:S(2)}) collective-permute-start(bf16[8,8,2,16,128]{4,3,2,1,0:T(8,128)(2,1)S(1)} %all-to-all-done.4.refs_5_), channel_id=1, source_target_pairs={{0,2},{1,3},{2,0},{3,1},{4,6},{5,7},{6,4},{7,5},{8,10},{9,11},{10,... | collective-permute-start | bytes 1572872 | tf_op jit(solution)/shard_map/ppermute | solution.py:39
  163.3 14.0 %collective-permute-start.8 = (bf16[8,8,2,16,128]{4,3,2,1,0:T(8,128)(2,1)S(1)}, bf16[8,8,2,16,128]{4,3,2,1,0:T(8,128)(2,1)S(1)}, u32[]{:S(2)}, u32[]{:S(2)}) collective-permute-start(bf16[8,8,2,16,128]{4,3,2,1,0:T(8,128)(2,1)S(1)} %all_to_all.33.refs_5_), channel_id=1, source_target_pairs={{0,1},{1,0},{2,3},{3,2},{4,5},{5,4},{6,7},{7,6},{8,9},{9,8},{10,11... | collective-permute-start | bytes 1572872 | tf_op jit(solution)/shard_map/ppermute | solution.py:39
  163.4 14.1 %copy-start.8 = (bf16[8,8,2,16,128]{4,3,2,1,0:T(8,128)(2,1)}, bf16[8,8,2,16,128]{4,3,2,1,0:T(8,128)(2,1)S(1)}, u32[]{:S(2)}) copy-start(bf16[8,8,2,16,128]{4,3,2,1,0:T(8,128)(2,1)S(1)} %collective-permute-done.7.refs_6_) | copy-start | bytes 1572868
  163.4 14.0 %collective-permute-start.9 = (bf16[8,8,2,16,128]{4,3,2,1,0:T(8,128)(2,1)S(1)}, bf16[8,8,2,16,128]{4,3,2,1,0:T(8,128)(2,1)}, u32[]{:S(2)}, u32[]{:S(2)}) collective-permute-start(bf16[8,8,2,16,128]{4,3,2,1,0:T(8,128)(2,1)S(1)} %collective-permute-done.7.refs_6_), channel_id=1, source_target_pairs={{0,1},{1,0},{2,3},{3,2},{4,5},{5,4},{6,7},{7,6},{8,9},{9,8},{10,11... | collective-permute-start | bytes 1572872 | tf_op jit(solution)/shard_map/ppermute | solution.py:39
  163.9 36.9 %collective-permute-start.5 = (bf16[8,8,2,16,128]{4,3,2,1,0:T(8,128)(2,1)S(1)}, bf16[8,8,2,16,128]{4,3,2,1,0:T(8,128)(2,1)S(1)}, u32[]{:S(2)}, u32[]{:S(2)}) collective-permute-start(bf16[8,8,2,16,128]{4,3,2,1,0:T(8,128)(2,1)S(1)} %all-to-all-done.4.refs_5_), channel_id=1, source_target_pairs={{0,1},{1,0},{2,3},{3,2},{4,5},{5,4},{6,7},{7,6},{8,9},{9,8},{10,11... | collective-permute-start | bytes 1572872 | tf_op jit(solution)/shard_map/ppermute | solution.py:39
  174.7 26.1 %copy-start.7 = (bf16[8,8,2,16,128]{4,3,2,1,0:T(8,128)(2,1)}, bf16[8,8,2,16,128]{4,3,2,1,0:T(8,128)(2,1)S(1)}, u32[]{:S(2)}) copy-start(bf16[8,8,2,16,128]{4,3,2,1,0:T(8,128)(2,1)S(1)} %collective-permute-done.4.refs_6_) | copy-start | bytes 1572868
  174.7 26.1 %collective-permute-start.6 = (bf16[8,8,2,16,128]{4,3,2,1,0:T(8,128)(2,1)S(1)}, bf16[8,8,2,16,128]{4,3,2,1,0:T(8,128)(2,1)}, u32[]{:S(2)}, u32[]{:S(2)}) collective-permute-start(bf16[8,8,2,16,128]{4,3,2,1,0:T(8,128)(2,1)S(1)} %collective-permute-done.4.refs_6_), channel_id=1, source_target_pairs={{0,1},{1,0},{2,3},{3,2},{4,5},{5,4},{6,7},{7,6},{8,9},{9,8},{10,11... | collective-permute-start | bytes 1572872 | tf_op jit(solution)/shard_map/ppermute | solution.py:39
  177.4 0.8 copy-start.10
  200.8 0.8 copy-start.9
  201.6 22.7 %copy-start.1 = (bf16[128]{0:T(256)(128)(2,1)S(1)}, bf16[128]{0:T(256)(128)(2,1)}, u32[]{:S(2)}) copy-start(bf16[128]{0:T(256)(128)(2,1)} %param.17) | copy-start | bytes 772
